TPU v7x, 256 devices: a whole 4x4x8 slice. The times are simulated.
256 devices in a mesh: ka: 8 (over z_hi, x), band: 32 (over y, z_lo, core).
Axes of the slice: x: 4, y: 4, z: 8 (z_hi: 2, z_lo: 4; z = z_hi * 4 + z_lo), core: 2. Of those that a mesh axis runs over, the one named last changes fastest.
Arguments:
- psi_hat: float32 [8, 12, 2, 128, 128, 128], P('ka', None, None, 'band'), may hold values from -1.5 to 1.5
- occupations: int32 [8, 12], P('ka'), may hold values from 0 to 2
- weights: int32 [8], P('ka'), may hold values from 1 to 6
- density_in: float32 [128, 128, 128], P('band'), may hold values from -12 to 12
- dens_hist: float32 [8, 128, 128, 128], P(None, 'band'), may hold values from -3 to 3
- resid_hist: float32 [8, 128, 128, 128], P(None, 'band'), may hold values from -12 to 12
Outputs:
- out_density: float32 [128, 128, 128], P('band')
- mixed_density: float32 [128, 128, 128], P('band')
All inputs are finite; a program needn't handle non-finite values.
Results may differ from a plain program's by a relative error of at most 0.0003.
Values sent between devices are 32-bit elements; how exact they have to be, the bound alone decides.
A program may use at most 128 MiB of HBM per device.

v0:
```python
from functools import partial

import jax
import jax.numpy as jnp
import ml_dtypes
import numpy as np
from jax import lax
from jax.experimental import pallas as pl
from jax.experimental.pallas import tpu as pltpu
from jax.sharding import PartitionSpec as P

NG = 128
BANDS = 12
HIST = 8
KA = 8
NB = 32
XS = 4
PLANES = NG // NB
REST = BANDS - 1
ROWS = REST * 8
QUARTER = NG // XS
CHUNKS = PLANES + 1
BETA = 0.3
REGULAR = 0.01
MESH = pl.DeviceIdType.MESH


def split_table(table):
    high = table.astype(ml_dtypes.bfloat16)
    low = (table - high.astype(np.float64)).astype(ml_dtypes.bfloat16)
    return high, low


def dft_tables():
    index = np.arange(NG)
    angles = 2.0 * np.pi * (index[:, None] * index[None, :] % NG) / NG
    cosine, sine = np.cos(angles), np.sin(angles)
    table = np.block([[cosine, -sine], [sine, cosine]])
    order = [
        part * NG + source * PLANES + p
        for source in range(NB)
        for part in range(2)
        for p in range(PLANES)
    ]
    return (*split_table(table), *split_table(table[:, order]))


def split(x):
    high = x.astype(jnp.bfloat16)
    low = (x - high.astype(jnp.float32)).astype(jnp.bfloat16)
    return high, low


def times(table_high, table_low, x, contract):
    high, low = split(x)
    dot = partial(
        lax.dot_general,
        dimension_numbers=(((1,), (contract,)), ((), ())),
        preferred_element_type=jnp.float32,
    )
    return dot(table_high, high) + (dot(table_low, high) + dot(table_high, low))


def diagonal_row(columns):
    sums = jnp.sum(columns, axis=1, keepdims=True)
    shape = columns.shape
    on = lax.broadcasted_iota(jnp.int32, shape, 0) == lax.broadcasted_iota(jnp.int32, shape, 1)
    return jnp.sum(jnp.where(on, sums, 0.0), axis=0, keepdims=True)


def spread_rows(row, count):
    shape = (count, 128)
    on = lax.broadcasted_iota(jnp.int32, shape, 0) == lax.broadcasted_iota(jnp.int32, shape, 1)
    picked = jnp.sum(jnp.where(on, row, 0.0), axis=1, keepdims=True)
    return jnp.broadcast_to(picked, shape)


def kernel(
    occ, weights, psi, din_hbm, dens_hbm, resid_hbm, th_hbm, tl_hbm, xh_hbm, xl_hbm,
    out_density, out_mixed,
    psi_v, din, dens, resid, th, tl, xh, xl,
    send_a, send_b, recv_a, recv_b,
    plane_buf, rs_buf, z_send, z_recv, gram_part, gram_rows, proj_rows, w_rows, chol,
    psi_sem, load_sem, own_sem,
    band_send, band_recv, rs_send, rs_recv, z_ssem, z_rsem, ag_send, ag_recv,
    gram_ssem, gram_rsem, proj_ssem, proj_rsem, w_ssem, w_rsem,
):
    ka = lax.axis_index("ka")
    me = lax.axis_index("band")
    z_hi, x = lax.div(ka, XS), lax.rem(ka, XS)
    y, z, core = lax.div(me, 8), lax.rem(lax.div(me, 2), 4), lax.rem(me, 2)

    def band_peer(n):
        step = NB - 1 - n
        dz, dy, dc = lax.div(step, 8), lax.rem(lax.div(step, 2), 4), lax.rem(step, 2)
        z_top = lax.rem(lax.div(z, 2) + lax.div(dz, 2), 2)
        z_low = lax.rem(z + dz, 2)
        return lax.rem(y + dy, 4) * 8 + (z_top * 2 + z_low) * 2 + lax.rem(core + dc, 2)

    def ka_peer(n):
        return lax.rem(ka + 1 + n, KA)

    def x_peer(n):
        return lax.rem(x + 1 + n, XS)

    def each(count, body):
        def step(n, carry):
            body(n)
            return carry

        lax.fori_loop(0, count, step, 0)

    def psi_load(b):
        return pltpu.make_async_copy(psi.at[0, b], psi_v.at[b], psi_sem.at[b])

    loads = [
        pltpu.make_async_copy(src, dst, load_sem.at[i])
        for i, (src, dst) in enumerate(
            [
                (th_hbm, th), (tl_hbm, tl), (xh_hbm, xh), (xl_hbm, xl),
                (resid_hbm, resid), (dens_hbm, dens), (din_hbm, din),
            ]
        )
    ]
    loads[0].start()
    loads[1].start()
    each(BANDS, lambda b: psi_load(b).start())
    for load in loads[2:]:
        load.start()

    barrier = pltpu.get_barrier_semaphore()

    def greet_band(n):
        pl.semaphore_signal(barrier, inc=1, device_id=(ka, band_peer(n)), device_id_type=MESH)

    def greet_ka(n):
        pl.semaphore_signal(barrier, inc=1, device_id=(ka_peer(n), me), device_id_type=MESH)

    each(NB - 1, greet_band)
    each(KA - 1, greet_ka)
    loads[0].wait()
    loads[1].wait()

    def transform(b, store):
        psi_load(b).wait()
        columns = jnp.concatenate(
            [
                jnp.concatenate([psi_v[b, 0, p], psi_v[b, 1, p]], axis=0)
                for p in range(PLANES)
            ],
            axis=1,
        )
        along_y = times(th[...], tl[...], columns, 0)
        rows = jnp.concatenate(
            [
                jnp.concatenate(
                    [
                        along_y[:NG, p * NG : (p + 1) * NG],
                        along_y[NG:, p * NG : (p + 1) * NG],
                    ],
                    axis=1,
                )
                for p in range(PLANES)
            ],
            axis=0,
        )
        along_z = times(th[...], tl[...], rows, 1)
        for part in range(2):
            for p in range(PLANES):
                store(
                    part * PLANES + p,
                    along_z[part * NG : (part + 1) * NG, p * NG : (p + 1) * NG],
                )

    def store_a(j, block):
        send_a[pl.ds(j, NG, stride=8), :] = block

    transform(0, store_a)
    pl.semaphore_wait(barrier, NB + KA - 2)

    def copy_a(n, peer, slot):
        return pltpu.make_async_remote_copy(
            src_ref=send_a.at[pl.ds(peer * 32, 32), :],
            dst_ref=recv_a.at[slot],
            send_sem=band_send.at[0, n],
            recv_sem=band_recv.at[0, slot],
            device_id=(ka, peer),
            device_id_type=MESH,
        )

    def copy_b(zi, n, peer, slot):
        return pltpu.make_async_remote_copy(
            src_ref=send_b.at[pl.ds((peer * PLANES + zi) * ROWS, ROWS), :],
            dst_ref=recv_b.at[zi * NB + slot],
            send_sem=band_send.at[zi + 1, n],
            recv_sem=band_recv.at[zi + 1, slot],
            device_id=(ka, peer),
            device_id_type=MESH,
        )

    def own_b(zi):
        return pltpu.make_async_copy(
            send_b.at[pl.ds((me * PLANES + zi) * ROWS, ROWS), :],
            recv_b.at[zi * NB + me],
            own_sem.at[zi + 1],
        )

    own_a = pltpu.make_async_copy(
        send_a.at[pl.ds(me * 32, 32), :], recv_a.at[me], own_sem.at[0]
    )

    each(NB - 1, lambda n: copy_a(n, band_peer(n), me).start())
    own_a.start()

    def store_b(b):
        def store(j, block):
            send_b[pl.ds((b - 1) * 8 + j, NG, stride=ROWS), :] = block

        return store

    each(REST, lambda i: transform(i + 1, store_b(i + 1)))

    def start_b(zi):
        each(NB - 1, lambda n: copy_b(zi, n, band_peer(n), me).start())
        own_b(zi).start()

    start_b(0)

    own_weight = jnp.full((1, 128), weights[0].astype(jnp.float32))
    w_rows[ka] = own_weight

    def w_copy(n, peer, slot):
        return pltpu.make_async_remote_copy(
            src_ref=w_rows.at[ka],
            dst_ref=w_rows.at[slot],
            send_sem=w_ssem.at[n],
            recv_sem=w_rsem.at[slot],
            device_id=(peer, me),
            device_id_type=MESH,
        )

    loads[4].wait()

    def gram_step(h):
        product = resid[h].reshape(1, PLANES * NG // 8, 8, NG) * resid[...].reshape(
            HIST, PLANES * NG // 8, 8, NG
        )
        gram_part[pl.ds(pl.multiple_of(h * HIST, HIST), HIST), :] = jnp.sum(
            jnp.sum(product, axis=1), axis=1
        )

    each(HIST, gram_step)
    each(KA - 1, lambda n: w_copy(n, ka_peer(n), ka).start())
    gram_rows[me] = diagonal_row(gram_part[...])

    def row_copy(rows, ssem, rsem, n, peer, slot):
        return pltpu.make_async_remote_copy(
            src_ref=rows.at[me],
            dst_ref=rows.at[slot],
            send_sem=ssem.at[n],
            recv_sem=rsem.at[slot],
            device_id=(ka, peer),
            device_id_type=MESH,
        )

    loads[5].wait()
    loads[6].wait()
    dens[...] = dens[...] + BETA * resid[...]

    start_b(1)
    gram_copy = partial(row_copy, gram_rows, gram_ssem, gram_rsem)
    each(NB - 1, lambda n: gram_copy(n, band_peer(n), me).start())

    each(KA - 1, lambda n: w_copy(n, ka_peer(n), ka_peer(n)).wait_recv())
    total_weight = jnp.sum(w_rows[...], axis=0)
    factor = own_weight / total_weight * jnp.float32(1.0 / NG**3)

    loads[2].wait()
    loads[3].wait()

    def operand_a(zi):
        return recv_a[:, pl.ds(pl.multiple_of(zi * 8, 8), 8), :].reshape(2 * NG, NG)

    def operand_b(zi, b):
        return recv_b[
            pl.ds(zi * NB, NB), pl.ds(pl.multiple_of((b - 1) * 8, 8), 8), :
        ].reshape(2 * NG, NG)

    def pair_power(left, right, b_left, b_right):
        field = times(xh[...], xl[...], jnp.concatenate([left, right], axis=1), 0)
        power = field[:NG] * field[:NG] + field[NG:] * field[NG:]
        return (
            power[:, :NG] * occ[0, b_left].astype(jnp.float32)
            + power[:, NG:] * occ[0, b_right].astype(jnp.float32)
        )

    def compute_plane(zi):
        plane_buf[zi] = pair_power(operand_a(zi), operand_b(zi, REST), 0, REST)

        def pair(i):
            b = 2 * i + 1
            plane_buf[zi] = plane_buf[zi] + pair_power(
                operand_b(zi, b), operand_b(zi, b + 1), b, b + 1
            )

        each(REST // 2, pair)
        plane_buf[zi] = plane_buf[zi] * factor

    def rs_copy(zi, n, peer, slot):
        return pltpu.make_async_remote_copy(
            src_ref=plane_buf.at[zi, pl.ds(peer * QUARTER, QUARTER), :],
            dst_ref=rs_buf.at[zi, slot],
            send_sem=rs_send.at[zi, n],
            recv_sem=rs_recv.at[zi, slot],
            device_id=(z_hi * XS + peer, me),
            device_id_type=MESH,
        )

    def z_copy(zi):
        return pltpu.make_async_remote_copy(
            src_ref=z_send.at[zi],
            dst_ref=z_recv.at[zi],
            send_sem=z_ssem.at[zi],
            recv_sem=z_rsem.at[zi],
            device_id=(lax.rem(ka + XS, KA), me),
            device_id_type=MESH,
        )

    def ag_copy(zi, n, peer, slot):
        mine = pl.ds(pl.multiple_of(x * QUARTER, QUARTER), QUARTER)
        return pltpu.make_async_remote_copy(
            src_ref=out_density.at[zi, mine, :],
            dst_ref=out_density.at[zi, mine, :],
            send_sem=ag_send.at[zi, n],
            recv_sem=ag_recv.at[zi, slot],
            device_id=(z_hi * XS + peer, me),
            device_id_type=MESH,
        )

    def gather_start(zi):
        z_copy(zi).wait_recv()
        mine = pl.ds(pl.multiple_of(x * QUARTER, QUARTER), QUARTER)
        out_density[zi, mine, :] = z_send[zi] + z_recv[zi]
        each(XS - 1, lambda n: ag_copy(zi, n, x_peer(n), x).start())

    def plane_step(zi):
        def arrived(n):
            peer = band_peer(n)
            copy_b(zi, n, peer, peer).wait_recv()

        each(NB - 1, arrived)
        own_b(zi).wait()
        compute_plane(zi)
        each(XS - 1, lambda n: rs_copy(zi, n, x_peer(n), x).start())

    def plane_finish(zi):
        each(XS - 1, lambda n: rs_copy(zi, n, x_peer(n), x_peer(n)).wait_recv())
        mine = pl.ds(pl.multiple_of(x * QUARTER, QUARTER), QUARTER)
        z_send[zi] = (
            plane_buf[zi, mine, :]
            + rs_buf[zi, lax.rem(x + 1, XS)]
            + rs_buf[zi, lax.rem(x + 2, XS)]
            + rs_buf[zi, lax.rem(x + 3, XS)]
        )
        z_copy(zi).start()

    def arrived_a(n):
        peer = band_peer(n)
        copy_a(n, peer, peer).wait_recv()

    each(NB - 1, arrived_a)
    own_a.wait()

    def early(zi):
        plane_step(zi)

        @pl.when(zi < PLANES - 2)
        def _():
            start_b(zi + 2)

        @pl.when(zi < PLANES - 1)
        def _():
            plane_finish(zi)

        @pl.when(zi == 1)
        def _():
            factorize()

    def factorize():
        each(NB - 1, lambda n: gram_copy(n, band_peer(n), band_peer(n)).wait_recv())
        gram_part[...] = spread_rows(jnp.sum(gram_rows[...], axis=0), HIST * HIST)

        def entry(i, j):
            return gram_part[i * HIST + j : i * HIST + j + 1, :]

        lower = {}
        for j in range(HIST):
            pivot = entry(j, j) * (1.0 + REGULAR)
            for k in range(j):
                pivot = pivot - lower[j, k] * lower[j, k]
            inverse = 1.0 / jnp.sqrt(pivot)
            chol[j * HIST + j : j * HIST + j + 1, :] = inverse
            for i in range(j + 1, HIST):
                value = entry(i, j)
                for k in range(j):
                    value = value - lower[i, k] * lower[j, k]
                lower[i, j] = value * inverse
                chol[i * HIST + j : i * HIST + j + 1, :] = lower[i, j]

    each(PLANES, early)

    last = PLANES - 1
    each(last, gather_start)
    plane_finish(last)
    gather_start(last)

    def gathered(zi):
        each(XS - 1, lambda n: ag_copy(zi, n, x_peer(n), x_peer(n)).wait_recv())

    each(PLANES, gathered)

    residual = out_density[...] - din[...]
    product = (resid[...] * residual[None]).reshape(HIST, PLANES * NG // 8, 8, NG)
    proj_rows[me] = diagonal_row(jnp.sum(jnp.sum(product, axis=1), axis=1))
    proj_copy = partial(row_copy, proj_rows, proj_ssem, proj_rsem)
    each(NB - 1, lambda n: proj_copy(n, band_peer(n), me).start())
    each(NB - 1, lambda n: proj_copy(n, band_peer(n), band_peer(n)).wait_recv())
    right = spread_rows(jnp.sum(proj_rows[...], axis=0), HIST)

    def factor_entry(i, j):
        return chol[i * HIST + j : i * HIST + j + 1, :]

    forward = []
    for i in range(HIST):
        value = right[i : i + 1, :]
        for j in range(i):
            value = value - factor_entry(i, j) * forward[j]
        forward.append(value * factor_entry(i, i))
    coefs = [None] * HIST
    for i in reversed(range(HIST)):
        value = forward[i]
        for j in range(i + 1, HIST):
            value = value - factor_entry(j, i) * coefs[j]
        coefs[i] = value * factor_entry(i, i)

    for zi in range(PLANES):
        mixed = din[zi] + BETA * (out_density[zi] - din[zi])
        update = coefs[0] * dens[0, zi]
        for h in range(1, HIST):
            update = update + coefs[h] * dens[h, zi]
        out_mixed[zi] = mixed - update

    each(NB - 1, lambda n: copy_a(n, band_peer(n), me).wait_send())
    each(
        PLANES,
        lambda zi: each(NB - 1, lambda n: copy_b(zi, n, band_peer(n), me).wait_send()),
    )
    each(NB - 1, lambda n: gram_copy(n, band_peer(n), me).wait_send())
    each(NB - 1, lambda n: proj_copy(n, band_peer(n), me).wait_send())
    each(KA - 1, lambda n: w_copy(n, ka_peer(n), ka).wait_send())

    def sent(zi):
        each(XS - 1, lambda n: rs_copy(zi, n, x_peer(n), x).wait_send())
        z_copy(zi).wait_send()
        each(XS - 1, lambda n: ag_copy(zi, n, x_peer(n), x).wait_send())

    each(PLANES, sent)


def shards(psi_hat, occupations, weights, density_in, dens_hist, resid_hist):
    th, tl, xh, xl = (jnp.asarray(table) for table in dft_tables())
    plane = (PLANES, NG, NG)
    f32 = jnp.float32
    dma = pltpu.SemaphoreType.DMA
    vmem = partial(pltpu.VMEM)
    any_spec = pl.BlockSpec(memory_space=pl.ANY)
    smem_spec = pl.BlockSpec(memory_space=pltpu.SMEM)
    vmem_spec = pl.BlockSpec(memory_space=pltpu.VMEM)
    table = vmem((2 * NG, 2 * NG), jnp.bfloat16)
    return pl.pallas_call(
        kernel,
        out_shape=(jax.ShapeDtypeStruct(plane, f32), jax.ShapeDtypeStruct(plane, f32)),
        in_specs=[smem_spec, smem_spec] + [any_spec] * 8,
        out_specs=(vmem_spec, vmem_spec),
        scratch_shapes=[
            vmem((BANDS, 2, PLANES, NG, NG), f32),
            vmem(plane, f32),
            vmem((HIST, *plane), f32),
            vmem((HIST, *plane), f32),
            table, table, table, table,
            vmem((NG * 8, NG), f32),
            vmem((NG * ROWS, NG), f32),
            vmem((NB, 8 * PLANES, NG), f32),
            vmem((PLANES * NB, ROWS, NG), f32),
            vmem(plane, f32),
            vmem((PLANES, XS, QUARTER, NG), f32),
            vmem((PLANES, QUARTER, NG), f32),
            vmem((PLANES, QUARTER, NG), f32),
            vmem((HIST * HIST, 128), f32),
            vmem((NB, 1, 128), f32),
            vmem((NB, 1, 128), f32),
            vmem((KA, 1, 128), f32),
            vmem((HIST * HIST, 128), f32),
            dma((BANDS,)), dma((7,)), dma((CHUNKS,)),
            dma((CHUNKS, NB)), dma((CHUNKS, NB)),
            dma((PLANES, XS)), dma((PLANES, XS)),
            dma((PLANES,)), dma((PLANES,)),
            dma((PLANES, XS)), dma((PLANES, XS)),
            dma((NB,)), dma((NB,)), dma((NB,)), dma((NB,)),
            dma((KA,)), dma((KA,)),
        ],
        compiler_params=pltpu.CompilerParams(
            collective_id=0, has_side_effects=True, vmem_limit_bytes=56 * 1024 * 1024
        ),
    )(occupations, weights, psi_hat, density_in, dens_hist, resid_hist, th, tl, xh, xl)


def solution(mesh):
    return jax.shard_map(
        shards,
        mesh=mesh,
        in_specs=(
            P("ka", None, None, "band", None, None),
            P("ka", None),
            P("ka"),
            P("band", None, None),
            P(None, "band", None, None),
            P(None, "band", None, None),
        ),
        out_specs=(P("band", None, None), P("band", None, None)),
        check_vma=False,
    )
```

profile of v0, /device:TPU:1, one launch (start us, length us, event | category | flops | bytes accessed | tf_op | source)
XLA Modules:
  0.0 184.8 jit_solution(14400390998434753393)
XLA Ops:
  1.3 180.2 %shard_map.113 = (f32[4,128,128]{2,1,0:T(8,128)}, f32[4,128,128]{2,1,0:T(8,128)}) custom-call(s32[1,12]{1,0:T(1,128)} %occ.1, s32[1]{0:T(128)S(6)} %copy.14.weights, f32[1,12,2,4,128,128]{5,4,3,2,1,0:T(8,128)} %psi.1, f32[4,128,128]{2,1,0:T(8,128)} %din_hbm.1, f32[8,4,128,128]{3,2,1,0:T(8,128)} %dens_hbm.1, f32[8,4,128,128]{3,2,1,0:T(8,128)} %resid_hbm.1, ...), custom_call_target="tpu_custom_call" | custom-call | tf_op jit(solution)/shard_map/pallas_call | solution.py:480
  181.5 1.7 copy.15
  183.2 1.7 copy.16
where the time goes:
time: 185 us
  Pallas kernels  180 us (97%)
  local copies, waits for them, and re-layouts  3.34 us (2%)
    pallas_call x1, Pallas kernels, shards(): pl.pallas_call(kernel, out_shape=(jax.ShapeDtypeStruct(plane, f32), jax.S...  180 us

commit v1 on v0

v1 whole, which is shorter than its diff:
```python
from functools import partial

import jax
import jax.numpy as jnp
import ml_dtypes
import numpy as np
from jax import lax
from jax.experimental import pallas as pl
from jax.experimental.pallas import tpu as pltpu
from jax.sharding import PartitionSpec as P

NG = 128
BANDS = 12
HIST = 8
KA = 8
NB = 32
XS = 4
PLANES = NG // NB
REST = BANDS - 1
ROWS = REST * 8
QUARTER = NG // XS
CHUNKS = PLANES + 1
BETA = 0.3
REGULAR = 0.01
MESH = pl.DeviceIdType.MESH


def split_table(table):
    high = table.astype(ml_dtypes.bfloat16)
    low = (table - high.astype(np.float64)).astype(ml_dtypes.bfloat16)
    return high, low


def dft_tables():
    index = np.arange(NG)
    angles = 2.0 * np.pi * (index[:, None] * index[None, :] % NG) / NG
    cosine, sine = np.cos(angles), np.sin(angles)
    table = np.block([[cosine, -sine], [sine, cosine]])
    order = [
        part * NG + source * PLANES + p
        for source in range(NB)
        for part in range(2)
        for p in range(PLANES)
    ]
    return (*split_table(table), *split_table(table[:, order]))


def split(x):
    high = x.astype(jnp.bfloat16)
    low = (x - high.astype(jnp.float32)).astype(jnp.bfloat16)
    return high, low


def times(table_high, table_low, x, contract):
    high, low = split(x)
    dot = partial(
        lax.dot_general,
        dimension_numbers=(((1,), (contract,)), ((), ())),
        preferred_element_type=jnp.float32,
    )
    return dot(table_high, high) + (dot(table_low, high) + dot(table_high, low))


def diagonal_row(columns):
    sums = jnp.sum(columns, axis=1, keepdims=True)
    shape = columns.shape
    on = lax.broadcasted_iota(jnp.int32, shape, 0) == lax.broadcasted_iota(jnp.int32, shape, 1)
    return jnp.sum(jnp.where(on, sums, 0.0), axis=0, keepdims=True)


def spread_rows(row, count):
    shape = (count, 128)
    on = lax.broadcasted_iota(jnp.int32, shape, 0) == lax.broadcasted_iota(jnp.int32, shape, 1)
    picked = jnp.sum(jnp.where(on, row, 0.0), axis=1, keepdims=True)
    return jnp.broadcast_to(picked, shape)


def kernel(
    weights, occ_hbm, psi, din_hbm, dens_hbm, resid_hbm, th_hbm, tl_hbm, xh_hbm, xl_hbm,
    out_density, out_mixed,
    occ, psi_v, din, dens, resid, th, tl, xh, xl,
    send_a, send_b, recv_a, recv_b,
    plane_buf, rs_buf, z_send, z_recv, gram_part, gram_rows, proj_part, proj_rows, total_rows, w_rows, inverse,
    psi_sem, load_sem, own_sem,
    band_send, band_recv, rs_send, rs_recv, z_ssem, z_rsem, ag_send, ag_recv,
    gram_sem, proj_sem, total_sem, w_sem,
):
    ka = lax.axis_index("ka")
    me = lax.axis_index("band")
    z_hi, x = lax.div(ka, XS), lax.rem(ka, XS)
    y, z, core = lax.div(me, 8), lax.rem(lax.div(me, 2), 4), lax.rem(me, 2)

    def band_peer(n):
        step = NB - 1 - n
        dz, dy, dc = lax.div(step, 8), lax.rem(lax.div(step, 2), 4), lax.rem(step, 2)
        z_top = lax.rem(lax.div(z, 2) + lax.div(dz, 2), 2)
        z_low = lax.rem(z + dz, 2)
        return lax.rem(y + dy, 4) * 8 + (z_top * 2 + z_low) * 2 + lax.rem(core + dc, 2)

    def ka_peer(n):
        return lax.rem(ka + 1 + n, KA)

    def x_peer(n):
        return lax.rem(x + 1 + n, XS)

    def each(count, body):
        def step(n, carry):
            body(n)
            return carry

        lax.fori_loop(0, count, step, 0)

    def wait_bytes(ref, sem):
        pltpu.make_async_copy(ref, ref, sem).wait()

    mine = pl.ds(pl.multiple_of(x * QUARTER, QUARTER), QUARTER)

    barrier = pltpu.get_barrier_semaphore()

    def greet_band(n):
        pl.semaphore_signal(barrier, inc=1, device_id=(ka, band_peer(n)), device_id_type=MESH)

    def greet_ka(n):
        pl.semaphore_signal(barrier, inc=1, device_id=(ka_peer(n), me), device_id_type=MESH)

    each(NB - 1, greet_band)
    each(KA - 1, greet_ka)

    first_psi = pltpu.make_async_copy(psi.at[0, 0], psi_v.at[0], psi_sem.at[0])
    other_psi = pltpu.make_async_copy(
        psi.at[0, pl.ds(1, REST)], psi_v.at[pl.ds(1, REST)], psi_sem.at[1]
    )
    loads = [
        pltpu.make_async_copy(src, dst, load_sem.at[i])
        for i, (src, dst) in enumerate(
            [
                (th_hbm, th), (tl_hbm, tl), (xh_hbm, xh), (xl_hbm, xl),
                (resid_hbm, resid), (dens_hbm, dens), (din_hbm, din),
                (occ_hbm, occ),
            ]
        )
    ]
    loads[0].start()
    loads[1].start()
    first_psi.start()
    other_psi.start()
    for load in loads[2:]:
        load.start()
    loads[0].wait()
    loads[1].wait()
    first_psi.wait()

    def transform(b, store):
        columns = jnp.concatenate(
            [
                jnp.concatenate([psi_v[b, 0, p], psi_v[b, 1, p]], axis=0)
                for p in range(PLANES)
            ],
            axis=1,
        )
        along_y = times(th[...], tl[...], columns, 0)
        rows = jnp.concatenate(
            [
                jnp.concatenate(
                    [
                        along_y[:NG, p * NG : (p + 1) * NG],
                        along_y[NG:, p * NG : (p + 1) * NG],
                    ],
                    axis=1,
                )
                for p in range(PLANES)
            ],
            axis=0,
        )
        along_z = times(th[...], tl[...], rows, 1)
        for part in range(2):
            for p in range(PLANES):
                store(
                    part * PLANES + p,
                    along_z[part * NG : (part + 1) * NG, p * NG : (p + 1) * NG],
                )

    def store_a(j, block):
        send_a[pl.ds(j, NG, stride=8), :] = block

    transform(0, store_a)
    pl.semaphore_wait(barrier, NB + KA - 2)

    def start_a(n):
        peer = band_peer(n)
        pltpu.make_async_remote_copy(
            src_ref=send_a.at[pl.ds(peer * 32, 32), :],
            dst_ref=recv_a.at[me],
            send_sem=band_send.at[0],
            recv_sem=band_recv.at[0],
            device_id=(ka, peer),
            device_id_type=MESH,
        ).start()

    own_a = pltpu.make_async_copy(
        send_a.at[pl.ds(me * 32, 32), :], recv_a.at[me], own_sem.at[0]
    )

    def own_b(zi):
        return pltpu.make_async_copy(
            send_b.at[pl.ds((me * PLANES + zi) * ROWS, ROWS), :],
            recv_b.at[zi * NB + me],
            own_sem.at[zi + 1],
        )

    def start_b(zi):
        def start(n):
            peer = band_peer(n)
            pltpu.make_async_remote_copy(
                src_ref=send_b.at[pl.ds((peer * PLANES + zi) * ROWS, ROWS), :],
                dst_ref=recv_b.at[zi * NB + me],
                send_sem=band_send.at[zi + 1],
                recv_sem=band_recv.at[zi + 1],
                device_id=(ka, peer),
                device_id_type=MESH,
            ).start()

        each(NB - 1, start)
        own_b(zi).start()

    def wait_b(zi, sems):
        wait_bytes(recv_b.at[pl.ds(zi * NB, NB - 1)], sems.at[zi + 1])

    def start_row(rows, sem, peer):
        pltpu.make_async_remote_copy(
            src_ref=rows.at[me],
            dst_ref=rows.at[me],
            send_sem=sem.at[0],
            recv_sem=sem.at[1],
            device_id=(ka, peer),
            device_id_type=MESH,
        ).start()

    def start_ka_row(rows, sem, peer):
        pltpu.make_async_remote_copy(
            src_ref=rows.at[ka],
            dst_ref=rows.at[ka],
            send_sem=sem.at[0],
            recv_sem=sem.at[1],
            device_id=(peer, me),
            device_id_type=MESH,
        ).start()

    def wait_rows(rows, count, sem, side):
        wait_bytes(rows.at[pl.ds(0, count - 1)], sem.at[side])

    each(NB - 1, start_a)
    own_a.start()

    def store_b(b):
        def store(j, block):
            send_b[pl.ds((b - 1) * 8 + j, NG, stride=ROWS), :] = block

        return store

    other_psi.wait()
    each(REST, lambda i: transform(i + 1, store_b(i + 1)))
    loads[7].wait()
    own_weight = jnp.full((1, 128), weights[0].astype(jnp.float32))
    w_rows[ka] = own_weight
    start_b(0)

    loads[4].wait()

    def gram_step(h):
        product = resid[h].reshape(1, PLANES * NG // 8, 8, NG) * resid[...].reshape(
            HIST, PLANES * NG // 8, 8, NG
        )
        gram_part[pl.ds(pl.multiple_of(h * HIST, HIST), HIST), :] = jnp.sum(
            jnp.sum(product, axis=1), axis=1
        )

    each(HIST, gram_step)
    each(KA - 1, lambda n: start_ka_row(w_rows, w_sem, ka_peer(n)))
    gram_rows[me] = diagonal_row(gram_part[...])

    loads[5].wait()
    loads[6].wait()
    dens[...] = dens[...] + BETA * resid[...]
    proj_part[...] = jnp.zeros((HIST, 128), jnp.float32)

    start_b(1)
    each(NB - 1, lambda n: start_row(gram_rows, gram_sem, band_peer(n)))

    wait_rows(w_rows, KA, w_sem, 1)
    factor = own_weight / jnp.sum(w_rows[...], axis=0) * jnp.float32(1.0 / NG**3)
    loads[2].wait()
    loads[3].wait()

    def operand_a(zi):
        return recv_a[:, pl.ds(pl.multiple_of(zi * 8, 8), 8), :].reshape(2 * NG, NG)

    def operand_b(zi, b):
        return recv_b[
            pl.ds(zi * NB, NB), pl.ds(pl.multiple_of((b - 1) * 8, 8), 8), :
        ].reshape(2 * NG, NG)

    def pair_power(left, right, b_left, b_right):
        field = times(xh[...], xl[...], jnp.concatenate([left, right], axis=1), 0)
        power = field[:NG] * field[:NG] + field[NG:] * field[NG:]
        return (
            power[:, :NG] * occ[0, b_left].astype(jnp.float32)
            + power[:, NG:] * occ[0, b_right].astype(jnp.float32)
        )

    def compute_plane(zi):
        plane_buf[zi] = pair_power(operand_a(zi), operand_b(zi, REST), 0, REST)

        def pair(i):
            b = 2 * i + 1
            plane_buf[zi] = plane_buf[zi] + pair_power(
                operand_b(zi, b), operand_b(zi, b + 1), b, b + 1
            )

        each(REST // 2, pair)
        plane_buf[zi] = plane_buf[zi] * factor

    def start_rs(zi):
        def start(n):
            peer = x_peer(n)
            pltpu.make_async_remote_copy(
                src_ref=plane_buf.at[zi, pl.ds(peer * QUARTER, QUARTER), :],
                dst_ref=rs_buf.at[zi, x],
                send_sem=rs_send.at[zi],
                recv_sem=rs_recv.at[zi],
                device_id=(z_hi * XS + peer, me),
                device_id_type=MESH,
            ).start()

        each(XS - 1, start)

    def z_copy(zi):
        return pltpu.make_async_remote_copy(
            src_ref=z_send.at[zi],
            dst_ref=z_recv.at[zi],
            send_sem=z_ssem.at[zi],
            recv_sem=z_rsem.at[zi],
            device_id=(lax.rem(ka + XS, KA), me),
            device_id_type=MESH,
        )

    def add_up(zi):
        wait_bytes(rs_buf.at[zi, pl.ds(0, XS - 1)], rs_recv.at[zi])
        z_send[zi] = (
            plane_buf[zi, mine, :]
            + rs_buf[zi, lax.rem(x + 1, XS)]
            + rs_buf[zi, lax.rem(x + 2, XS)]
            + rs_buf[zi, lax.rem(x + 3, XS)]
        )
        z_copy(zi).start()

    def start_gather(zi):
        z_copy(zi).wait_recv()
        out_density[zi, mine, :] = z_send[zi] + z_recv[zi]

        def start(n):
            pltpu.make_async_remote_copy(
                src_ref=out_density.at[zi, mine, :],
                dst_ref=out_density.at[zi, mine, :],
                send_sem=ag_send.at[zi],
                recv_sem=ag_recv.at[zi],
                device_id=(z_hi * XS + x_peer(n), me),
                device_id_type=MESH,
            ).start()

        each(XS - 1, start)

    def project(zi):
        own = plane_buf[zi] - (1.0 / KA) * din[zi]
        product = (resid[:, zi] * own[None]).reshape(HIST, NG // 8, 8, NG)
        proj_part[...] = proj_part[...] + jnp.sum(jnp.sum(product, axis=1), axis=1)

    def plane_step(zi):
        wait_b(zi, band_recv)
        own_b(zi).wait()
        compute_plane(zi)
        start_rs(zi)
        project(zi)

    def invert():
        wait_rows(gram_rows, NB, gram_sem, 1)
        gram_part[...] = spread_rows(jnp.sum(gram_rows[...], axis=0), HIST * HIST)

        def entry(i, j):
            return gram_part[i * HIST + j : i * HIST + j + 1, :]

        lower, pivots = {}, []
        for j in range(HIST):
            pivot = entry(j, j) * (1.0 + REGULAR)
            for k in range(j):
                pivot = pivot - lower[j, k] * lower[j, k]
            pivots.append(1.0 / jnp.sqrt(pivot))
            for i in range(j + 1, HIST):
                value = entry(i, j)
                for k in range(j):
                    value = value - lower[i, k] * lower[j, k]
                lower[i, j] = value * pivots[j]
        unlower = {}
        for j in range(HIST):
            unlower[j, j] = pivots[j]
            for i in range(j + 1, HIST):
                value = lower[i, j] * unlower[j, j]
                for k in range(j + 1, i):
                    value = value + lower[i, k] * unlower[k, j]
                unlower[i, j] = -value * pivots[i]
        lane = lax.broadcasted_iota(jnp.int32, (1, 128), 1)
        for i in range(HIST):
            row = jnp.zeros((1, 128), jnp.float32)
            for j in range(HIST):
                value = sum(unlower[k, i] * unlower[k, j] for k in range(max(i, j), HIST))
                row = jnp.where(lane == j, value, row)
            inverse[i : i + 1, :] = row

    def early(zi):
        plane_step(zi)
        add_up(zi)

        @pl.when(zi < PLANES - 2)
        def _():
            start_b(zi + 2)

        @pl.when(zi > 0)
        def _():
            start_gather(zi - 1)

        @pl.when(zi == 1)
        def _():
            invert()

    last = PLANES - 1
    wait_bytes(recv_a.at[pl.ds(0, NB - 1)], band_recv.at[0])
    own_a.wait()
    each(last, early)

    wait_bytes(recv_a.at[pl.ds(0, NB - 1)], band_send.at[0])
    for zi in range(PLANES - 2):
        wait_b(zi, band_send)
    wait_rows(w_rows, KA, w_sem, 0)
    wait_rows(gram_rows, NB, gram_sem, 0)

    plane_step(last)
    proj_rows[me] = diagonal_row(proj_part[...])
    each(NB - 1, lambda n: start_row(proj_rows, proj_sem, band_peer(n)))
    add_up(last)
    start_gather(last - 1)
    wait_rows(proj_rows, NB, proj_sem, 1)
    total_rows[ka] = jnp.sum(proj_rows[...], axis=0)
    each(KA - 1, lambda n: start_ka_row(total_rows, total_sem, ka_peer(n)))
    start_gather(last)

    for zi in range(PLANES - 2, PLANES):
        wait_b(zi, band_send)
    wait_rows(proj_rows, NB, proj_sem, 0)
    for zi in range(PLANES):
        wait_bytes(rs_buf.at[zi, pl.ds(0, XS - 1)], rs_send.at[zi])
        z_copy(zi).wait_send()

    wait_rows(total_rows, KA, total_sem, 1)
    projections = jnp.sum(total_rows[...], axis=0)
    coefs = jnp.sum(inverse[...] * projections, axis=1, keepdims=True)
    for zi in range(PLANES):
        wait_bytes(out_density.at[zi, pl.ds(0, NG - QUARTER), :], ag_recv.at[zi])
        update = coefs[0:1] * dens[0, zi]
        for h in range(1, HIST):
            update = update + coefs[h : h + 1] * dens[h, zi]
        out_mixed[zi] = din[zi] + BETA * (out_density[zi] - din[zi]) - update

    wait_rows(total_rows, KA, total_sem, 0)
    for zi in range(PLANES):
        wait_bytes(out_density.at[zi, pl.ds(0, NG - QUARTER), :], ag_send.at[zi])


def shards(psi_hat, occupations, weights, density_in, dens_hist, resid_hist):
    operands = (occupations, psi_hat, density_in, dens_hist, resid_hist)
    operands += tuple(jnp.asarray(table) for table in dft_tables())
    plane = (PLANES, NG, NG)
    f32 = jnp.float32
    dma = pltpu.SemaphoreType.DMA
    vmem = partial(pltpu.VMEM)
    hbm_spec = pl.BlockSpec(memory_space=pltpu.HBM)
    vmem_spec = pl.BlockSpec(memory_space=pltpu.VMEM)
    table = vmem((2 * NG, 2 * NG), jnp.bfloat16)
    return pl.pallas_call(
        kernel,
        out_shape=(jax.ShapeDtypeStruct(plane, f32), jax.ShapeDtypeStruct(plane, f32)),
        in_specs=[pl.BlockSpec(memory_space=pltpu.SMEM)] + [hbm_spec] * 9,
        out_specs=(vmem_spec, vmem_spec),
        scratch_shapes=[
            pltpu.SMEM((1, BANDS), jnp.int32),
            vmem((BANDS, 2, PLANES, NG, NG), f32),
            vmem(plane, f32),
            vmem((HIST, *plane), f32),
            vmem((HIST, *plane), f32),
            table, table, table, table,
            vmem((NG * 8, NG), f32),
            vmem((NG * ROWS, NG), f32),
            vmem((NB, 8 * PLANES, NG), f32),
            vmem((PLANES * NB, ROWS, NG), f32),
            vmem(plane, f32),
            vmem((PLANES, XS, QUARTER, NG), f32),
            vmem((PLANES, QUARTER, NG), f32),
            vmem((PLANES, QUARTER, NG), f32),
            vmem((HIST * HIST, 128), f32),
            vmem((NB, 1, 128), f32),
            vmem((HIST, 128), f32),
            vmem((NB, 1, 128), f32),
            vmem((KA, 1, 128), f32),
            vmem((KA, 1, 128), f32),
            vmem((HIST, 128), f32),
            dma((2,)), dma((8,)), dma((CHUNKS,)),
            dma((CHUNKS,)), dma((CHUNKS,)),
            dma((PLANES,)), dma((PLANES,)),
            dma((PLANES,)), dma((PLANES,)),
            dma((PLANES,)), dma((PLANES,)),
            dma((2,)), dma((2,)), dma((2,)), dma((2,)),
        ],
        compiler_params=pltpu.CompilerParams(
            collective_id=0, has_side_effects=True, vmem_limit_bytes=32 * 1024 * 1024
        ),
    )(weights, *(pltpu.with_memory_space_constraint(operand, pltpu.HBM) for operand in operands))


def solution(mesh):
    return jax.shard_map(
        shards,
        mesh=mesh,
        in_specs=(
            P("ka", None, None, "band", None, None),
            P("ka", None),
            P("ka"),
            P("band", None, None),
            P(None, "band", None, None),
            P(None, "band", None, None),
        ),
        out_specs=(P("band", None, None), P("band", None, None)),
        check_vma=False,
    )
```

time: 185 us -> 169 us (0.914)
  Pallas kernels: 180 us -> 166 us
  local copies, waits for them, and re-layouts: 3.34 us -> 1.41 us
    pallas_call x1, Pallas kernels: 180 us -> 166 us  [shards(): pl.pallas_call(kernel, out_shape=(jax.ShapeDtypeStruct(plane, f32), jax.S...]
    unnamed x2, local copies, waits for them, and re-layouts: 3.34 us -> 1.41 us
where the time goes in v1:
time: 169 us
  Pallas kernels  166 us (98%)
    pallas_call x1, Pallas kernels, shards(): pl.pallas_call(kernel, out_shape=(jax.ShapeDtypeStruct(plane, f32), jax.S...  166 us

profile of v1, /device:TPU:1, one launch (start us, length us, event | category | flops | bytes accessed | tf_op | source)
XLA Modules:
  0.0 169.0 jit_solution(10266567645868628869)
XLA Ops:
  1.3 166.3 %shard_map.113 = (f32[4,128,128]{2,1,0:T(8,128)S(1)}, f32[4,128,128]{2,1,0:T(8,128)S(1)}) custom-call(s32[1]{0:T(128)S(6)} %copy.14.weights, s32[1,12]{1,0:T(1,128)} %occ_hbm.1, f32[1,12,2,4,128,128]{5,4,3,2,1,0:T(8,128)} %psi.1, f32[4,128,128]{2,1,0:T(8,128)} %din_hbm.1, f32[8,4,128,128]{3,2,1,0:T(8,128)} %dens_hbm.1, f32[8,4,128,128]{3,2,1,0:T(8,128)} %resid_hbm.1, ...), custom_call_target="tpu_custom_call" | custom-call | tf_op jit(solution)/shard_map/pallas_call | solution.py:488
  167.5 0.7 copy.15
  168.2 0.7 copy.16

commit v2 on v1

--- a/solution.py
+++ b/solution.py
@@ -19,7 +19,8 @@
 REST = BANDS - 1
 ROWS = REST * 8
 QUARTER = NG // XS
-CHUNKS = PLANES + 1
+LATE = 3
+CHUNKS = PLANES + 2
 BETA = 0.3
 REGULAR = 0.01
 MESH = pl.DeviceIdType.MESH
@@ -97,6 +98,16 @@
         z_low = lax.rem(z + dz, 2)
         return lax.rem(y + dy, 4) * 8 + (z_top * 2 + z_low) * 2 + lax.rem(core + dc, 2)
 
+    y_part = [lax.rem(y + dy, 4) * 8 for dy in range(4)]
+    z_part = [
+        lax.rem(lax.div(z, 2) + dz // 2, 2) * 4 + lax.rem(z + dz, 2) * 2 for dz in range(4)
+    ]
+    core_part = [core, 1 - core]
+    band_peers = [
+        y_part[step // 2 % 4] + z_part[step // 8] + core_part[step % 2]
+        for step in range(NB - 1, 0, -1)
+    ]
+
     def ka_peer(n):
         return lax.rem(ka + 1 + n, KA)
 
@@ -113,18 +124,8 @@
     def wait_bytes(ref, sem):
         pltpu.make_async_copy(ref, ref, sem).wait()
 
+    last = PLANES - 1
     mine = pl.ds(pl.multiple_of(x * QUARTER, QUARTER), QUARTER)
-
-    barrier = pltpu.get_barrier_semaphore()
-
-    def greet_band(n):
-        pl.semaphore_signal(barrier, inc=1, device_id=(ka, band_peer(n)), device_id_type=MESH)
-
-    def greet_ka(n):
-        pl.semaphore_signal(barrier, inc=1, device_id=(ka_peer(n), me), device_id_type=MESH)
-
-    each(NB - 1, greet_band)
-    each(KA - 1, greet_ka)
 
     first_psi = pltpu.make_async_copy(psi.at[0, 0], psi_v.at[0], psi_sem.at[0])
     other_psi = pltpu.make_async_copy(
@@ -141,8 +142,15 @@
         )
     ]
     loads[0].start()
+    first_psi.start()
     loads[1].start()
-    first_psi.start()
+
+    barrier = pltpu.get_barrier_semaphore()
+    for n in range(KA - 1):
+        pl.semaphore_signal(barrier, inc=1, device_id=(ka_peer(n), me), device_id_type=MESH)
+    for peer in band_peers:
+        pl.semaphore_signal(barrier, inc=1, device_id=(ka, peer), device_id_type=MESH)
+
     other_psi.start()
     for load in loads[2:]:
         load.start()
@@ -208,23 +216,35 @@
             own_sem.at[zi + 1],
         )
 
-    def start_b(zi):
+    def start_part(zi, sem, first, count):
+        rows = pl.ds(first * 8, count * 8)
+
         def start(n):
             peer = band_peer(n)
             pltpu.make_async_remote_copy(
-                src_ref=send_b.at[pl.ds((peer * PLANES + zi) * ROWS, ROWS), :],
-                dst_ref=recv_b.at[zi * NB + me],
-                send_sem=band_send.at[zi + 1],
-                recv_sem=band_recv.at[zi + 1],
+                src_ref=send_b.at[
+                    pl.ds((peer * PLANES + zi) * ROWS + first * 8, count * 8), :
+                ],
+                dst_ref=recv_b.at[zi * NB + me, rows],
+                send_sem=band_send.at[sem],
+                recv_sem=band_recv.at[sem],
                 device_id=(ka, peer),
                 device_id_type=MESH,
             ).start()
 
         each(NB - 1, start)
+
+    def wait_part(zi, sems, sem, first, count):
+        wait_bytes(
+            recv_b.at[pl.ds(zi * NB, NB - 1), pl.ds(first * 8, count * 8)], sems.at[sem]
+        )
+
+    def start_b(zi):
+        start_part(zi, zi + 1, 0, REST)
         own_b(zi).start()
 
     def wait_b(zi, sems):
-        wait_bytes(recv_b.at[pl.ds(zi * NB, NB - 1)], sems.at[zi + 1])
+        wait_part(zi, sems, zi + 1, 0, REST)
 
     def start_row(rows, sem, peer):
         pltpu.make_async_remote_copy(
@@ -319,6 +339,26 @@
 
         each(REST // 2, pair)
         plane_buf[zi] = plane_buf[zi] * factor
+
+    def compute_last_plane(zi):
+        wait_part(zi, band_recv, zi + 1, 0, REST - LATE)
+        own_b(zi).wait()
+        plane_buf[zi] = pair_power(operand_b(zi, 1), operand_b(zi, 2), 1, 2)
+
+        def pair(i):
+            b = 2 * i + 1
+            plane_buf[zi] = plane_buf[zi] + pair_power(
+                operand_b(zi, b), operand_b(zi, b + 1), b, b + 1
+            )
+
+        lax.fori_loop(1, (REST - LATE) // 2, lambda i, carry: (pair(i), carry)[1], 0)
+        wait_part(zi, band_recv, zi + 2, REST - LATE, LATE)
+        total = (
+            plane_buf[zi]
+            + pair_power(operand_b(zi, REST - 2), operand_b(zi, REST - 1), REST - 2, REST - 1)
+            + pair_power(operand_a(zi), operand_b(zi, REST), 0, REST)
+        )
+        plane_buf[zi] = total * factor
 
     def start_rs(zi):
         def start(n):
@@ -375,12 +415,6 @@
         product = (resid[:, zi] * own[None]).reshape(HIST, NG // 8, 8, NG)
         proj_part[...] = proj_part[...] + jnp.sum(jnp.sum(product, axis=1), axis=1)
 
-    def plane_step(zi):
-        wait_b(zi, band_recv)
-        own_b(zi).wait()
-        compute_plane(zi)
-        start_rs(zi)
-        project(zi)
 
     def invert():
         wait_rows(gram_rows, NB, gram_sem, 1)
@@ -417,12 +451,22 @@
             inverse[i : i + 1, :] = row
 
     def early(zi):
-        plane_step(zi)
+        wait_b(zi, band_recv)
+        own_b(zi).wait()
+        compute_plane(zi)
+        start_rs(zi)
+        project(zi)
         add_up(zi)
 
-        @pl.when(zi < PLANES - 2)
+        @pl.when(zi == 0)
         def _():
-            start_b(zi + 2)
+            start_b(2)
+
+        @pl.when(zi == 1)
+        def _():
+            start_part(last, last + 1, 0, REST - LATE)
+            own_b(last).start()
+            start_part(last, last + 2, REST - LATE, LATE)
 
         @pl.when(zi > 0)
         def _():
@@ -432,7 +476,6 @@
         def _():
             invert()
 
-    last = PLANES - 1
     wait_bytes(recv_a.at[pl.ds(0, NB - 1)], band_recv.at[0])
     own_a.wait()
     each(last, early)
@@ -443,9 +486,12 @@
     wait_rows(w_rows, KA, w_sem, 0)
     wait_rows(gram_rows, NB, gram_sem, 0)
 
-    plane_step(last)
+    compute_last_plane(last)
+    start_rs(last)
+    project(last)
     proj_rows[me] = diagonal_row(proj_part[...])
-    each(NB - 1, lambda n: start_row(proj_rows, proj_sem, band_peer(n)))
+    for peer in band_peers:
+        start_row(proj_rows, proj_sem, peer)
     add_up(last)
     start_gather(last - 1)
     wait_rows(proj_rows, NB, proj_sem, 1)
@@ -453,8 +499,9 @@
     each(KA - 1, lambda n: start_ka_row(total_rows, total_sem, ka_peer(n)))
     start_gather(last)
 
-    for zi in range(PLANES - 2, PLANES):
-        wait_b(zi, band_send)
+    wait_b(last - 1, band_send)
+    wait_part(last, band_send, last + 1, 0, REST - LATE)
+    wait_part(last, band_send, last + 2, REST - LATE, LATE)
     wait_rows(proj_rows, NB, proj_sem, 0)
     for zi in range(PLANES):
         wait_bytes(rs_buf.at[zi, pl.ds(0, XS - 1)], rs_send.at[zi])
@@ -473,6 +520,17 @@
     wait_rows(total_rows, KA, total_sem, 0)
     for zi in range(PLANES):
         wait_bytes(out_density.at[zi, pl.ds(0, NG - QUARTER), :], ag_send.at[zi])
+
+
+def write_out(density, mixed, out_density, out_mixed, sems):
+    copies = [
+        pltpu.make_async_copy(density, out_density, sems.at[0]),
+        pltpu.make_async_copy(mixed, out_mixed, sems.at[1]),
+    ]
+    for copy in copies:
+        copy.start()
+    for copy in copies:
+        copy.wait()
 
 
 def shards(psi_hat, occupations, weights, density_in, dens_hist, resid_hist):
@@ -485,7 +543,7 @@
     hbm_spec = pl.BlockSpec(memory_space=pltpu.HBM)
     vmem_spec = pl.BlockSpec(memory_space=pltpu.VMEM)
     table = vmem((2 * NG, 2 * NG), jnp.bfloat16)
-    return pl.pallas_call(
+    density, mixed = pl.pallas_call(
         kernel,
         out_shape=(jax.ShapeDtypeStruct(plane, f32), jax.ShapeDtypeStruct(plane, f32)),
         in_specs=[pl.BlockSpec(memory_space=pltpu.SMEM)] + [hbm_spec] * 9,
@@ -523,6 +581,14 @@
             collective_id=0, has_side_effects=True, vmem_limit_bytes=32 * 1024 * 1024
         ),
     )(weights, *(pltpu.with_memory_space_constraint(operand, pltpu.HBM) for operand in operands))
+    return pl.pallas_call(
+        write_out,
+        out_shape=(jax.ShapeDtypeStruct(plane, f32), jax.ShapeDtypeStruct(plane, f32)),
+        in_specs=[vmem_spec, vmem_spec],
+        out_specs=(hbm_spec, hbm_spec),
+        scratch_shapes=[dma((2,))],
+        compiler_params=pltpu.CompilerParams(vmem_limit_bytes=1024 * 1024),
+    )(density, mixed)
 
 
 def solution(mesh):

time: 169 us -> 167 us (0.988)
    pallas_call x1, Pallas kernels: 166 us -> 164 us  [shards(): pl.pallas_call(kernel, out_shape=(jax.ShapeDtypeStruct(plane, f32), jax.S...]
where the time goes in v2:
time: 167 us; the launch traced here: 166 us
  Pallas kernels  165 us (99%)
    pallas_call x1, Pallas kernels, shards(): pl.pallas_call(kernel, out_shape=(jax.ShapeDtypeStruct(plane, f32), jax.S...  164 us

profile of v2, /device:TPU:1, one launch (start us, length us, event | category | flops | bytes accessed | tf_op | source)
XLA Modules:
  0.0 166.4 jit_solution(18044799014156522096)
XLA Ops:
  1.3 164.3 %shard_map.113 = (f32[4,128,128]{2,1,0:T(8,128)S(1)}, f32[4,128,128]{2,1,0:T(8,128)S(1)}) custom-call(s32[1]{0:T(128)S(6)} %copy.12.weights, s32[1,12]{1,0:T(1,128)} %occ_hbm.1, f32[1,12,2,4,128,128]{5,4,3,2,1,0:T(8,128)} %psi.1, f32[4,128,128]{2,1,0:T(8,128)} %din_hbm.1, f32[8,4,128,128]{3,2,1,0:T(8,128)} %dens_hbm.1, f32[8,4,128,128]{3,2,1,0:T(8,128)} %resid_hbm.1, ...), custom_call_target="tpu_custom_call" | custom-call | tf_op jit(solution)/shard_map/pallas_call | solution.py:546
  165.5 0.8 shard_map.114

commit v3 on v2

--- a/solution.py
+++ b/solution.py
@@ -91,22 +91,35 @@
     z_hi, x = lax.div(ka, XS), lax.rem(ka, XS)
     y, z, core = lax.div(me, 8), lax.rem(lax.div(me, 2), 4), lax.rem(me, 2)
 
+    half = lax.div(z, 2)
+    z_end, z_middle, z_beside = 3 - 3 * half, 2 - half, half * 2 + 1 - lax.rem(z, 2)
+
     def band_peer(n):
-        step = NB - 1 - n
-        dz, dy, dc = lax.div(step, 8), lax.rem(lax.div(step, 2), 4), lax.rem(step, 2)
-        z_top = lax.rem(lax.div(z, 2) + lax.div(dz, 2), 2)
-        z_low = lax.rem(z + dz, 2)
-        return lax.rem(y + dy, 4) * 8 + (z_top * 2 + z_low) * 2 + lax.rem(core + dc, 2)
+        i, dy = lax.div(n, 4), 3 - lax.rem(n, 4)
+        z_far = jnp.where(lax.rem(i, 2) == 0, z_end, z_middle)
+        z_near = jnp.where(i < 6, z_beside, z)
+        core_near = jnp.where(i < 6, i - 4, jnp.where(i == 6, 1 - core, core))
+        z_to = jnp.where(i < 4, z_far, z_near)
+        core_to = jnp.where(i < 4, lax.div(i, 2), core_near)
+        return lax.rem(y + dy, 4) * 8 + z_to * 2 + core_to
 
     y_part = [lax.rem(y + dy, 4) * 8 for dy in range(4)]
-    z_part = [
-        lax.rem(lax.div(z, 2) + dz // 2, 2) * 4 + lax.rem(z + dz, 2) * 2 for dz in range(4)
-    ]
     core_part = [core, 1 - core]
-    band_peers = [
-        y_part[step // 2 % 4] + z_part[step // 8] + core_part[step % 2]
-        for step in range(NB - 1, 0, -1)
-    ]
+    others_along_z = [z_end, z_middle, z_beside]
+
+    def across(dx, dy, dc):
+        return z_hi * XS + lax.rem(x + dx, XS), y_part[dy] + z * 2 + core_part[dc]
+
+    flat = [(dx, dy, dc) for dx in range(XS) for dy in range(4) for dc in range(2)][1:]
+    flat_peers = [across(*step) for step in flat]
+    flat_slot = x * 8 + y * 2 + core
+    z_slot = z_hi * 4 + z
+
+    def along_z(dz):
+        to = lax.rem(z_slot + dz, 8)
+        return lax.div(to, 4) * XS + x, y * 8 + lax.rem(to, 4) * 2 + core
+
+    z_peers = [along_z(dz) for dz in range(1, 8)]
 
     def ka_peer(n):
         return lax.rem(ka + 1 + n, KA)
@@ -146,10 +159,16 @@
     loads[1].start()
 
     barrier = pltpu.get_barrier_semaphore()
-    for n in range(KA - 1):
-        pl.semaphore_signal(barrier, inc=1, device_id=(ka_peer(n), me), device_id_type=MESH)
-    for peer in band_peers:
-        pl.semaphore_signal(barrier, inc=1, device_id=(ka, peer), device_id_type=MESH)
+    for device in z_peers + flat_peers:
+        pl.semaphore_signal(barrier, inc=1, device_id=device, device_id_type=MESH)
+    other_half = XS - z_hi * XS
+    for dx in range(1, XS):
+        device = (other_half + lax.rem(x + dx, XS), me)
+        pl.semaphore_signal(barrier, inc=1, device_id=device, device_id_type=MESH)
+    for z_to in others_along_z:
+        for dy, dc in [(dy, dc) for dy in range(4) for dc in range(2)][1:]:
+            device = (ka, y_part[dy] + z_to * 2 + core_part[dc])
+            pl.semaphore_signal(barrier, inc=1, device_id=device, device_id_type=MESH)
 
     other_psi.start()
     for load in loads[2:]:
@@ -192,7 +211,7 @@
         send_a[pl.ds(j, NG, stride=8), :] = block
 
     transform(0, store_a)
-    pl.semaphore_wait(barrier, NB + KA - 2)
+    pl.semaphore_wait(barrier, 7 + NB - 1 + XS - 1 + 21)
 
     def start_a(n):
         peer = band_peer(n)
@@ -246,23 +265,13 @@
     def wait_b(zi, sems):
         wait_part(zi, sems, zi + 1, 0, REST)
 
-    def start_row(rows, sem, peer):
+    def start_slot(rows, slot, sem, device):
         pltpu.make_async_remote_copy(
-            src_ref=rows.at[me],
-            dst_ref=rows.at[me],
+            src_ref=rows.at[slot],
+            dst_ref=rows.at[slot],
             send_sem=sem.at[0],
             recv_sem=sem.at[1],
-            device_id=(ka, peer),
-            device_id_type=MESH,
-        ).start()
-
-    def start_ka_row(rows, sem, peer):
-        pltpu.make_async_remote_copy(
-            src_ref=rows.at[ka],
-            dst_ref=rows.at[ka],
-            send_sem=sem.at[0],
-            recv_sem=sem.at[1],
-            device_id=(peer, me),
+            device_id=device,
             device_id_type=MESH,
         ).start()
 
@@ -296,7 +305,7 @@
         )
 
     each(HIST, gram_step)
-    each(KA - 1, lambda n: start_ka_row(w_rows, w_sem, ka_peer(n)))
+    each(KA - 1, lambda n: start_slot(w_rows, ka, w_sem, (ka_peer(n), me)))
     gram_rows[me] = diagonal_row(gram_part[...])
 
     loads[5].wait()
@@ -305,7 +314,7 @@
     proj_part[...] = jnp.zeros((HIST, 128), jnp.float32)
 
     start_b(1)
-    each(NB - 1, lambda n: start_row(gram_rows, gram_sem, band_peer(n)))
+    each(NB - 1, lambda n: start_slot(gram_rows, me, gram_sem, (ka, band_peer(n))))
 
     wait_rows(w_rows, KA, w_sem, 1)
     factor = own_weight / jnp.sum(w_rows[...], axis=0) * jnp.float32(1.0 / NG**3)
@@ -489,14 +498,15 @@
     compute_last_plane(last)
     start_rs(last)
     project(last)
-    proj_rows[me] = diagonal_row(proj_part[...])
-    for peer in band_peers:
-        start_row(proj_rows, proj_sem, peer)
+    proj_rows[flat_slot] = diagonal_row(proj_part[...])
+    for device in flat_peers:
+        start_slot(proj_rows, flat_slot, proj_sem, device)
     add_up(last)
     start_gather(last - 1)
     wait_rows(proj_rows, NB, proj_sem, 1)
-    total_rows[ka] = jnp.sum(proj_rows[...], axis=0)
-    each(KA - 1, lambda n: start_ka_row(total_rows, total_sem, ka_peer(n)))
+    total_rows[z_slot] = jnp.sum(proj_rows[...], axis=0)
+    for device in z_peers:
+        start_slot(total_rows, z_slot, total_sem, device)
     start_gather(last)
 
     wait_b(last - 1, band_send)

time: 167 us -> 164 us (0.982)
  Pallas kernels: 165 us -> 163 us
    pallas_call x1, Pallas kernels: 164 us -> 162 us  [shards(): pl.pallas_call(kernel, out_shape=(jax.ShapeDtypeStruct(plane, f32), jax.S...]
where the time goes in v3:
time: 164 us
  Pallas kernels  163 us (99%)
    pallas_call x1, Pallas kernels, shards(): pl.pallas_call(kernel, out_shape=(jax.ShapeDtypeStruct(plane, f32), jax.S...  162 us

profile of v3, /device:TPU:1, one launch (start us, length us, event | category | flops | bytes accessed | tf_op | source)
XLA Modules:
  0.0 163.9 jit_solution(2603662689477792636)
XLA Ops:
  1.3 161.8 %shard_map.113 = (f32[4,128,128]{2,1,0:T(8,128)S(1)}, f32[4,128,128]{2,1,0:T(8,128)S(1)}) custom-call(s32[1]{0:T(128)S(6)} %copy.12.weights, s32[1,12]{1,0:T(1,128)} %occ_hbm.1, f32[1,12,2,4,128,128]{5,4,3,2,1,0:T(8,128)} %psi.1, f32[4,128,128]{2,1,0:T(8,128)} %din_hbm.1, f32[8,4,128,128]{3,2,1,0:T(8,128)} %dens_hbm.1, f32[8,4,128,128]{3,2,1,0:T(8,128)} %resid_hbm.1, ...), custom_call_target="tpu_custom_call" | custom-call | tf_op jit(solution)/shard_map/pallas_call | solution.py:556
  163.1 0.8 shard_map.114

commit v4 on v3

--- a/solution.py
+++ b/solution.py
@@ -362,6 +362,7 @@
 
         lax.fori_loop(1, (REST - LATE) // 2, lambda i, carry: (pair(i), carry)[1], 0)
         wait_part(zi, band_recv, zi + 2, REST - LATE, LATE)
+        each(last, lambda early_zi: z_copy(early_zi).start())
         total = (
             plane_buf[zi]
             + pair_power(operand_b(zi, REST - 2), operand_b(zi, REST - 1), REST - 2, REST - 1)
@@ -401,7 +402,6 @@
             + rs_buf[zi, lax.rem(x + 2, XS)]
             + rs_buf[zi, lax.rem(x + 3, XS)]
         )
-        z_copy(zi).start()
 
     def start_gather(zi):
         z_copy(zi).wait_recv()
@@ -477,10 +477,6 @@
             own_b(last).start()
             start_part(last, last + 2, REST - LATE, LATE)
 
-        @pl.when(zi > 0)
-        def _():
-            start_gather(zi - 1)
-
         @pl.when(zi == 1)
         def _():
             invert()
@@ -502,7 +498,8 @@
     for device in flat_peers:
         start_slot(proj_rows, flat_slot, proj_sem, device)
     add_up(last)
-    start_gather(last - 1)
+    z_copy(last).start()
+    each(last, start_gather)
     wait_rows(proj_rows, NB, proj_sem, 1)
     total_rows[z_slot] = jnp.sum(proj_rows[...], axis=0)
     for device in z_peers:

time: 164 us -> 162 us (0.988)
  Pallas kernels: 163 us -> 161 us
    pallas_call x1, Pallas kernels: 162 us -> 160 us  [shards(): pl.pallas_call(kernel, out_shape=(jax.ShapeDtypeStruct(plane, f32), jax.S...]
where the time goes in v4:
time: 162 us
  Pallas kernels  161 us (99%)
    pallas_call x1, Pallas kernels, shards(): pl.pallas_call(kernel, out_shape=(jax.ShapeDtypeStruct(plane, f32), jax.S...  160 us

profile of v4, /device:TPU:1, one launch (start us, length us, event | category | flops | bytes accessed | tf_op | source)
XLA Modules:
  0.0 161.9 jit_solution(12805005683242015866)
XLA Ops:
  1.3 159.8 %shard_map.113 = (f32[4,128,128]{2,1,0:T(8,128)S(1)}, f32[4,128,128]{2,1,0:T(8,128)S(1)}) custom-call(s32[1]{0:T(128)S(6)} %copy.12.weights, s32[1,12]{1,0:T(1,128)} %occ_hbm.1, f32[1,12,2,4,128,128]{5,4,3,2,1,0:T(8,128)} %psi.1, f32[4,128,128]{2,1,0:T(8,128)} %din_hbm.1, f32[8,4,128,128]{3,2,1,0:T(8,128)} %dens_hbm.1, f32[8,4,128,128]{3,2,1,0:T(8,128)} %resid_hbm.1, ...), custom_call_target="tpu_custom_call" | custom-call | tf_op jit(solution)/shard_map/pallas_call | solution.py:553
  161.1 0.8 shard_map.114

commit v5 on v4

--- a/solution.py
+++ b/solution.py
@@ -124,9 +124,6 @@
     def ka_peer(n):
         return lax.rem(ka + 1 + n, KA)
 
-    def x_peer(n):
-        return lax.rem(x + 1 + n, XS)
-
     def each(count, body):
         def step(n, carry):
             body(n)
@@ -159,16 +156,16 @@
     loads[1].start()
 
     barrier = pltpu.get_barrier_semaphore()
-    for device in z_peers + flat_peers:
-        pl.semaphore_signal(barrier, inc=1, device_id=device, device_id_type=MESH)
+    for z_to in others_along_z:
+        for dy, dc in [(dy, dc) for dy in range(4) for dc in range(2)][1:]:
+            device = (ka, y_part[dy] + z_to * 2 + core_part[dc])
+            pl.semaphore_signal(barrier, inc=1, device_id=device, device_id_type=MESH)
     other_half = XS - z_hi * XS
     for dx in range(1, XS):
         device = (other_half + lax.rem(x + dx, XS), me)
         pl.semaphore_signal(barrier, inc=1, device_id=device, device_id_type=MESH)
-    for z_to in others_along_z:
-        for dy, dc in [(dy, dc) for dy in range(4) for dc in range(2)][1:]:
-            device = (ka, y_part[dy] + z_to * 2 + core_part[dc])
-            pl.semaphore_signal(barrier, inc=1, device_id=device, device_id_type=MESH)
+    for device in z_peers + flat_peers:
+        pl.semaphore_signal(barrier, inc=1, device_id=device, device_id_type=MESH)
 
     other_psi.start()
     for load in loads[2:]:
@@ -362,7 +359,7 @@
 
         lax.fori_loop(1, (REST - LATE) // 2, lambda i, carry: (pair(i), carry)[1], 0)
         wait_part(zi, band_recv, zi + 2, REST - LATE, LATE)
-        each(last, lambda early_zi: z_copy(early_zi).start())
+        z_copy(0).start()
         total = (
             plane_buf[zi]
             + pair_power(operand_b(zi, REST - 2), operand_b(zi, REST - 1), REST - 2, REST - 1)
@@ -371,25 +368,25 @@
         plane_buf[zi] = total * factor
 
     def start_rs(zi):
-        def start(n):
-            peer = x_peer(n)
+        for dx in (2, 1, 3):
+            device = across(dx, 0, 0)
             pltpu.make_async_remote_copy(
-                src_ref=plane_buf.at[zi, pl.ds(peer * QUARTER, QUARTER), :],
+                src_ref=plane_buf.at[zi, pl.ds(lax.rem(x + dx, XS) * QUARTER, QUARTER), :],
                 dst_ref=rs_buf.at[zi, x],
                 send_sem=rs_send.at[zi],
                 recv_sem=rs_recv.at[zi],
-                device_id=(z_hi * XS + peer, me),
+                device_id=device,
                 device_id_type=MESH,
             ).start()
 
-        each(XS - 1, start)
-
-    def z_copy(zi):
+    groups = [pl.ds(0, last), pl.ds(last, 1)]
+
+    def z_copy(group):
         return pltpu.make_async_remote_copy(
-            src_ref=z_send.at[zi],
-            dst_ref=z_recv.at[zi],
-            send_sem=z_ssem.at[zi],
-            recv_sem=z_rsem.at[zi],
+            src_ref=z_send.at[groups[group]],
+            dst_ref=z_recv.at[groups[group]],
+            send_sem=z_ssem.at[group],
+            recv_sem=z_rsem.at[group],
             device_id=(lax.rem(ka + XS, KA), me),
             device_id_type=MESH,
         )
@@ -403,21 +400,22 @@
             + rs_buf[zi, lax.rem(x + 3, XS)]
         )
 
-    def start_gather(zi):
-        z_copy(zi).wait_recv()
-        out_density[zi, mine, :] = z_send[zi] + z_recv[zi]
-
-        def start(n):
+    def start_gather(group):
+        planes = groups[group]
+        z_copy(group).wait_recv()
+        out_density[planes, mine, :] = z_send[planes] + z_recv[planes]
+        for dx in (2, 1, 3):
             pltpu.make_async_remote_copy(
-                src_ref=out_density.at[zi, mine, :],
-                dst_ref=out_density.at[zi, mine, :],
-                send_sem=ag_send.at[zi],
-                recv_sem=ag_recv.at[zi],
-                device_id=(z_hi * XS + x_peer(n), me),
+                src_ref=out_density.at[planes, mine, :],
+                dst_ref=out_density.at[planes, mine, :],
+                send_sem=ag_send.at[group],
+                recv_sem=ag_recv.at[group],
+                device_id=across(dx, 0, 0),
                 device_id_type=MESH,
             ).start()
 
-        each(XS - 1, start)
+    def wait_gather(group, sems):
+        wait_bytes(out_density.at[groups[group], pl.ds(0, NG - QUARTER), :], sems.at[group])
 
     def project(zi):
         own = plane_buf[zi] - (1.0 / KA) * din[zi]
@@ -498,13 +496,13 @@
     for device in flat_peers:
         start_slot(proj_rows, flat_slot, proj_sem, device)
     add_up(last)
-    z_copy(last).start()
-    each(last, start_gather)
+    z_copy(1).start()
+    start_gather(0)
     wait_rows(proj_rows, NB, proj_sem, 1)
     total_rows[z_slot] = jnp.sum(proj_rows[...], axis=0)
     for device in z_peers:
         start_slot(total_rows, z_slot, total_sem, device)
-    start_gather(last)
+    start_gather(1)
 
     wait_b(last - 1, band_send)
     wait_part(last, band_send, last + 1, 0, REST - LATE)
@@ -512,21 +510,23 @@
     wait_rows(proj_rows, NB, proj_sem, 0)
     for zi in range(PLANES):
         wait_bytes(rs_buf.at[zi, pl.ds(0, XS - 1)], rs_send.at[zi])
-        z_copy(zi).wait_send()
+    z_copy(0).wait_send()
+    z_copy(1).wait_send()
 
     wait_rows(total_rows, KA, total_sem, 1)
     projections = jnp.sum(total_rows[...], axis=0)
     coefs = jnp.sum(inverse[...] * projections, axis=1, keepdims=True)
     for zi in range(PLANES):
-        wait_bytes(out_density.at[zi, pl.ds(0, NG - QUARTER), :], ag_recv.at[zi])
+        if zi == 0 or zi == last:
+            wait_gather(zi // last, ag_recv)
         update = coefs[0:1] * dens[0, zi]
         for h in range(1, HIST):
             update = update + coefs[h : h + 1] * dens[h, zi]
         out_mixed[zi] = din[zi] + BETA * (out_density[zi] - din[zi]) - update
 
     wait_rows(total_rows, KA, total_sem, 0)
-    for zi in range(PLANES):
-        wait_bytes(out_density.at[zi, pl.ds(0, NG - QUARTER), :], ag_send.at[zi])
+    wait_gather(0, ag_send)
+    wait_gather(1, ag_send)
 
 
 def write_out(density, mixed, out_density, out_mixed, sems):
@@ -580,8 +580,7 @@
             dma((2,)), dma((8,)), dma((CHUNKS,)),
             dma((CHUNKS,)), dma((CHUNKS,)),
             dma((PLANES,)), dma((PLANES,)),
-            dma((PLANES,)), dma((PLANES,)),
-            dma((PLANES,)), dma((PLANES,)),
+            dma((2,)), dma((2,)), dma((2,)), dma((2,)),
             dma((2,)), dma((2,)), dma((2,)), dma((2,)),
         ],
         compiler_params=pltpu.CompilerParams(

time: 162 us -> 162 us (level)
  no operation moved by 1% of the time
where the time goes in v5:
time: 162 us
  Pallas kernels  160 us (99%)
    pallas_call x1, Pallas kernels, shards(): pl.pallas_call(kernel, out_shape=(jax.ShapeDtypeStruct(plane, f32), jax.S...  160 us

profile of v5, /device:TPU:1, one launch (start us, length us, event | category | flops | bytes accessed | tf_op | source)
XLA Modules:
  0.0 161.6 jit_solution(18093616565916537508)
XLA Ops:
  1.3 159.5 %shard_map.113 = (f32[4,128,128]{2,1,0:T(8,128)S(1)}, f32[4,128,128]{2,1,0:T(8,128)S(1)}) custom-call(s32[1]{0:T(128)S(6)} %copy.12.weights, s32[1,12]{1,0:T(1,128)} %occ_hbm.1, f32[1,12,2,4,128,128]{5,4,3,2,1,0:T(8,128)} %psi.1, f32[4,128,128]{2,1,0:T(8,128)} %din_hbm.1, f32[8,4,128,128]{3,2,1,0:T(8,128)} %dens_hbm.1, f32[8,4,128,128]{3,2,1,0:T(8,128)} %resid_hbm.1, ...), custom_call_target="tpu_custom_call" | custom-call | tf_op jit(solution)/shard_map/pallas_call | solution.py:553
  160.8 0.8 shard_map.114

commit v6 on v5

--- a/solution.py
+++ b/solution.py
@@ -497,11 +497,11 @@
         start_slot(proj_rows, flat_slot, proj_sem, device)
     add_up(last)
     z_copy(1).start()
-    start_gather(0)
     wait_rows(proj_rows, NB, proj_sem, 1)
     total_rows[z_slot] = jnp.sum(proj_rows[...], axis=0)
     for device in z_peers:
         start_slot(total_rows, z_slot, total_sem, device)
+    start_gather(0)
     start_gather(1)
 
     wait_b(last - 1, band_send)

time: 162 us -> 162 us (level)
  no operation moved by 1% of the time
where the time goes in v6:
time: 162 us
  Pallas kernels  160 us (99%)
    pallas_call x1, Pallas kernels, shards(): pl.pallas_call(kernel, out_shape=(jax.ShapeDtypeStruct(plane, f32), jax.S...  160 us

profile of v6, /device:TPU:1, one launch (start us, length us, event | category | flops | bytes accessed | tf_op | source)
XLA Modules:
  0.0 161.6 jit_solution(12437781814128334684)
XLA Ops:
  1.3 159.5 %shard_map.113 = (f32[4,128,128]{2,1,0:T(8,128)S(1)}, f32[4,128,128]{2,1,0:T(8,128)S(1)}) custom-call(s32[1]{0:T(128)S(6)} %copy.12.weights, s32[1,12]{1,0:T(1,128)} %occ_hbm.1, f32[1,12,2,4,128,128]{5,4,3,2,1,0:T(8,128)} %psi.1, f32[4,128,128]{2,1,0:T(8,128)} %din_hbm.1, f32[8,4,128,128]{3,2,1,0:T(8,128)} %dens_hbm.1, f32[8,4,128,128]{3,2,1,0:T(8,128)} %resid_hbm.1, ...), custom_call_target="tpu_custom_call" | custom-call | tf_op jit(solution)/shard_map/pallas_call | solution.py:553
  160.8 0.8 shard_map.114
